TPU v7x, 256 devices: a whole 4x4x8 slice. The times are simulated.
256 devices in a mesh: seq: 64 (over x, y, z_lo, core), tp: 4 (over z_hi).
Axes of the slice: x: 4, y: 4, z: 8 (z_hi: 4, z_lo: 2; z = z_hi * 2 + z_lo), core: 2. Of those that a mesh axis runs over, the one named last changes fastest.
Arguments:
- hidden_in: bfloat16 [32768, 2048], P('seq', 'tp'), may hold values from -60 to 60
- w_query: bfloat16 [2048, 2048], P(None, 'tp'), may hold values from -0.125 to 0.125
- w_key: bfloat16 [2048, 2048], P(None, 'tp'), may hold values from -0.125 to 0.125
- w_value: bfloat16 [2048, 2048], P(None, 'tp'), may hold values from -0.8984375 to 0.8984375
- w_pos: bfloat16 [2048, 2048], P(None, 'tp'), may hold values from -0.125 to 0.125
- w_out: bfloat16 [2048, 2048], P('tp'), may hold values from -0.125 to 0.125
- bias_content: float32 [16, 128], P('tp'), may hold values from -4 to 4
- bias_pos: float32 [16, 128], P('tp'), may hold values from -4 to 4
- norm_gain: float32 [2048], P('tp'), may hold values from 0.1 to 1.9
- norm_bias: float32 [2048], P('tp'), may hold values from -3 to 3
Outputs:
- hidden_out: bfloat16 [32768, 2048], P('seq', 'tp')
All inputs are finite; a program needn't handle non-finite values.
Results may differ from a plain program's by a relative error of at most 0.014.
The roundings to bfloat16 on the way count: a program that leaves them out, or rounds other values in their place, can miss the bound.
Values may be sent and summed in bfloat16 or wider, within the bound.
A program may use at most 128 MiB of HBM per device.

v0:
```python
import jax
import jax.numpy as jnp
from jax import lax
from jax.sharding import PartitionSpec as P


def copy_for_each(x, axis):
    peers = lax.axis_size(axis)
    return lax.all_to_all(jnp.broadcast_to(x[None], (peers, *x.shape)), axis, 0, 0, tiled=True)


def in_order(parts, dim):
    parts = jnp.moveaxis(parts, 0, dim)
    dims = parts.shape
    return parts.reshape(*dims[:dim], dims[dim] * dims[dim + 1], *dims[dim + 2 :])


def gather_directly(x, axis, dim):
    parts = copy_for_each(x, axis)
    return in_order(parts, dim)


def shifted(block, axis, distance):
    devices = range(lax.axis_size(axis))
    route = [(i - distance, i) for i in devices if i - distance in devices]
    return lax.ppermute(block, axis, route)


def in_blocks(x, dim, peers):
    dims = x.shape
    parts = x.reshape(*dims[:dim], peers, dims[dim] // peers, *dims[dim + 1 :])
    return jnp.moveaxis(parts, dim, 0)


def sent_and_summed(x, axis, dim):
    parts = in_blocks(x, dim, lax.axis_size(axis))
    arrived = lax.all_to_all(parts, axis, split_axis=0, concat_axis=0, tiled=True)
    return arrived.astype(jnp.float32).sum(axis=0)


def taken_together(x, axis):
    everything = copy_for_each(x, axis)
    return jnp.sum(everything, axis=0)


def in_one(arrays, axis):
    ravelled, at, done = (jnp.concatenate([a.reshape(-1) for a in arrays]), 0, [])
    subtotal = taken_together(ravelled, axis)
    for a in arrays:
        done.append(subtotal[at : at + a.size].reshape(a.shape))
        at += a.size
    return tuple(done)


def relative_table(span, width):
    half = width // 2
    freq = jnp.exp(-jnp.log(10000.0) * jnp.arange(half).astype(jnp.float32) / half)
    distance = (span - 1 - jnp.arange(span)).astype(jnp.float32)
    angle = distance[:, None] * freq[None, :]
    return jnp.concatenate([jnp.sin(angle), jnp.cos(angle)], 1).astype(jnp.bfloat16)


def shift_rows(table, seg, span):
    heads = table.shape[0]
    padded = jnp.pad(table, ((0, 0), (0, 0), (0, 1)))
    flat = padded.reshape(heads, seg * (span + 1))
    return flat[:, seg - 1 : seg - 1 + seg * span].reshape(heads, seg, span)


def shards(
    hidden_in, w_query, w_key, w_value, w_pos, w_out, bias_content, bias_pos, norm_gain, norm_bias
):
    seg = hidden_in.shape[0]
    heads = bias_content.shape[0]
    head_dim = bias_content.shape[1]
    width = heads * head_dim
    model_width = w_query.shape[0]
    span = 3 * seg
    memory = 2 * seg
    place = lax.axis_index("seq")
    own = gather_directly(hidden_in, "tp", 1)
    query = jnp.dot(own, w_query, preferred_element_type=jnp.float32).astype(jnp.bfloat16)
    own_keys = jnp.dot(own, w_key, preferred_element_type=jnp.float32).astype(jnp.bfloat16)
    own_values = jnp.dot(own, w_value, preferred_element_type=jnp.float32).astype(jnp.bfloat16)
    key_parts = []
    value_parts = []
    for distance in (2, 1):
        earlier_keys, earlier_values = shifted((own_keys, own_values), "seq", distance)
        key_parts.append(earlier_keys)
        value_parts.append(earlier_values)
    keys = jnp.concatenate(key_parts + [own_keys], 0)
    values = jnp.concatenate(value_parts + [own_values], 0)
    rel = jnp.dot(
        relative_table(span, model_width), w_pos, preferred_element_type=jnp.float32
    ).astype(jnp.bfloat16)
    rel = rel.reshape(span, heads, head_dim)
    keys = keys.reshape(span, heads, head_dim)
    values = values.reshape(span, heads, head_dim)
    q_rows = query.astype(jnp.float32).reshape(seg, heads, head_dim)
    content_q = (q_rows + bias_content[None]).astype(jnp.bfloat16)
    pos_q = (q_rows + bias_pos[None]).astype(jnp.bfloat16)
    content = jnp.einsum("ihd,jhd->hij", content_q, keys, preferred_element_type=jnp.float32)
    position = jnp.einsum("ihd,ehd->hie", pos_q, rel, preferred_element_type=jnp.float32)
    position = shift_rows(position, seg, span)
    score = (content + position) * (1.0 / jnp.sqrt(jnp.float32(head_dim)))
    row = jnp.arange(seg)[:, None]
    col = jnp.arange(span)[None, :]
    allowed = (col <= row + memory) & (place * seg - memory + col >= 0)
    score = jnp.where(allowed[None], score, jnp.float32(-1e30))
    probs = jax.nn.softmax(score, axis=-1).astype(jnp.bfloat16)
    attended = jnp.einsum("hij,jhd->ihd", probs, values, preferred_element_type=jnp.float32)
    attended = attended.astype(jnp.bfloat16).reshape(seg, width)
    partial_out = jnp.dot(attended, w_out, preferred_element_type=jnp.float32)
    branch = sent_and_summed(partial_out.astype(jnp.bfloat16), "tp", 1)
    summed = hidden_in.astype(jnp.float32) + branch
    total, squares = in_one((jnp.sum(summed, axis=1), jnp.sum(summed * summed, axis=1)), "tp")
    center = total / model_width
    spread = squares / model_width - center * center
    centred = summed - center[:, None]
    normed = centred / jnp.sqrt(spread[:, None] + 1e-05)
    return (normed * norm_gain[None] + norm_bias[None]).astype(jnp.bfloat16)


def solution(mesh):
    in_specs = (
        P("seq", "tp"),
        P(None, "tp"),
        P(None, "tp"),
        P(None, "tp"),
        P(None, "tp"),
        P("tp", None),
        P("tp", None),
        P("tp", None),
        P("tp"),
        P("tp"),
    )
    out_specs = P("seq", "tp")
    return jax.shard_map(shards, mesh=mesh, in_specs=in_specs, out_specs=out_specs, check_vma=False)
```

profile of v0, /device:TPU:6, one launch (start us, length us, event | category | flops | bytes accessed | tf_op | source)
XLA Modules:
  0.0 257.6 jit_solution(13610870744949388573)
XLA Ops:
  0.0 0.0 copy-start
  0.0 1.4 copy.36
  1.4 1.5 broadcast_in_dim.12
  2.9 8.5 %all-to-all-start = ((bf16[4,512,512]{1,2,0:T(8,128)(2,1)}), bf16[4,512,512]{1,2,0:T(8,128)(2,1)}, u32[]{:S(2)}, u32[]{:S(2)}) async-start(bf16[4,512,512]{1,2,0:T(8,128)(2,1)} %broadcast_in_dim.12), calls=%async_computation | async-start | bytes 4194304 | tf_op jit(solution)/shard_map/all_to_all | solution.py:9
  11.4 0.6 fusion.10
  11.9 0.0 copy-start.8
  12.0 23.2 %fusion.3 = (bf16[1536,1024]{1,0:T(8,128)(2,1)S(1)}, bf16[1536,1024]{1,0:T(8,128)(2,1)S(1)}) fusion(f32[1024]{0:T(1024)S(1)} %multiply_exponential_fusion, f32[1536]{0:T(1024)S(1)} %subtract_convert_fusion), kind=kLoop, calls=%fused_computation.8 | loop fusion | flops 4718592 | bytes 6301696 | tf_op jit(solution)/shard_map/convert.1
  35.2 0.0 copy-done.8
  35.2 4.9 %fusion.11 = bf16[1536,512]{0,1:T(8,128)(2,1)} fusion(bf16[2048,512]{1,0:T(8,128)(2,1)S(1)} %copy-done.8, bf16[1536,1024]{1,0:T(8,128)(2,1)S(1)} %get-tuple-element.8, bf16[1536,1024]{1,0:T(8,128)(2,1)S(1)} %get-tuple-element.7), kind=kOutput, calls=%fused_computation.18 | convolution fusion | flops 3234594816 | bytes 9961472 | tf_op jit(solution)/shard_map/dot_general | solution.py:93
  40.1 22.2 %all-to-all-done = bf16[4,512,512]{1,2,0:T(8,128)(2,1)} async-done(((bf16[4,512,512]{1,2,0:T(8,128)(2,1)}), bf16[4,512,512]{1,2,0:T(8,128)(2,1)}, u32[]{:S(2)}, u32[]{:S(2)}) %all-to-all-start) | async-done | bytes 2097184 | tf_op jit(solution)/shard_map/all_to_all | solution.py:9
  62.2 0.0 copy-start.3
  62.2 3.6 %convolution_convert_fusion.1 = bf16[512,512]{1,0:T(8,128)(2,1)S(1)} fusion(bf16[512,2048]{0,1:T(8,128)(2,1)} %bitcast.1, bf16[2048,512]{1,0:T(8,128)(2,1)} %param.12), kind=kOutput, calls=%fused_computation.25 | convolution fusion | flops 1074003968 | bytes 4718592 | tf_op jit(solution)/shard_map/dot_general | solution.py:83
  65.9 0.0 copy-start.9
  65.9 3.0 %collective-permute-start.2 = (bf16[512,512]{1,0:T(8,128)(2,1)S(1)}, bf16[512,512]{1,0:T(8,128)(2,1)}, u32[]{:S(2)}, u32[]{:S(2)}) collective-permute-start(bf16[512,512]{1,0:T(8,128)(2,1)S(1)} %convolution_convert_fusion.1), channel_id=1, source_target_pairs={{0,8},{4,12},{8,16},{12,20},{16,24},{20,28},{24,32},{28,36},{32,40... | collective-permute-start | bytes 1572872 | tf_op jit(solution)/shard_map/ppermute | solution.py:26
  68.9 1.9 collective-permute-start.3
  70.8 0.0 copy-done.3
  70.9 3.7 %convolution_convert_fusion.3 = bf16[512,512]{1,0:T(8,128)(2,1)} fusion(bf16[512,2048]{0,1:T(8,128)(2,1)} %bitcast.1, bf16[2048,512]{1,0:T(8,128)(2,1)S(1)} %copy-done.3), kind=kOutput, calls=%fused_computation.27 | convolution fusion | flops 1074003968 | bytes 4718592 | tf_op jit(solution)/shard_map/dot_general | solution.py:84
  74.5 0.0 copy-start.4
  74.5 4.1 %collective-permute-start = (bf16[512,512]{1,0:T(8,128)(2,1)}, bf16[512,512]{1,0:T(8,128)(2,1)}, u32[]{:S(2)}, u32[]{:S(2)}) collective-permute-start(bf16[512,512]{1,0:T(8,128)(2,1)} %convolution_convert_fusion.3), channel_id=1, source_target_pairs={{0,8},{4,12},{8,16},{12,20},{16,24},{20,28},{24,32},{28,36},{32,40... | collective-permute-start | bytes 1572872 | tf_op jit(solution)/shard_map/ppermute | solution.py:26
  78.6 2.7 %collective-permute-start.1 = (bf16[512,512]{1,0:T(8,128)(2,1)}, bf16[512,512]{1,0:T(8,128)(2,1)}, u32[]{:S(2)}, u32[]{:S(2)}) collective-permute-start(bf16[512,512]{1,0:T(8,128)(2,1)} %convolution_convert_fusion.3), channel_id=1, source_target_pairs={{0,4},{4,8},{8,12},{12,16},{16,20},{20,24},{24,28},{28,32},{32,36}... | collective-permute-start | bytes 1572872 | tf_op jit(solution)/shard_map/ppermute | solution.py:26
  81.3 0.0 copy-done.9
  81.3 3.7 %convolution_convert_fusion.2 = bf16[512,512]{0,1:T(8,128)(2,1)} fusion(bf16[512,2048]{0,1:T(8,128)(2,1)} %bitcast.1, bf16[2048,512]{1,0:T(8,128)(2,1)S(1)} %copy-done.9), kind=kOutput, calls=%fused_computation.26 | convolution fusion | flops 1074003968 | bytes 4718592 | tf_op jit(solution)/shard_map/dot_general | solution.py:82
  85.0 2.2 copy.37
  87.2 0.0 copy-done.4
  87.2 8.1 %fusion.17 = f32[4,512,1536]{2,1,0:T(8,128)} fusion(bf16[1536,4,128]{0,2,1:T(8,128)(2,1)} %bitcast.46, f32[512,4,128]{2,0,1:T(8,128)} %copy.37, f32[4,128]{1,0:T(4,128)S(1)} %copy-done.4), kind=kOutput, calls=%fused_computation.34 | convolution fusion | flops 805830656 | bytes 15206400 | tf_op jit(solution)/shard_map/ihd,ehd->hie/dot_general | solution.py:103
  95.3 10.8 %pad.4 = f32[4,512,1537]{2,1,0:T(8,128)} pad(f32[4,512,1536]{2,1,0:T(8,128)} %fusion.17, f32[]{:T(128)} %constant.13.clone.1), padding=0_0x0_0x0_1 | pad | bytes 25174020 | tf_op jit(solution)/shard_map/jit(_pad)/pad | solution.py:65
  106.1 20.2 %reshape.116 = f32[3147776]{0:T(1024)} reshape(f32[4,512,1537]{2,1,0:T(8,128)} %pad.4) | data formatting | bytes 25182208
  126.3 15.0 %reshape.110 = f32[4,786944]{1,0:T(4,128)} reshape(f32[3147776]{0:T(1024)} %reshape.116) | data formatting | bytes 25182208 | tf_op jit(solution)/shard_map/reshape | solution.py:66
  141.3 0.0 copy-start.1
  141.3 0.0 copy-start.5
  141.3 9.7 %slice.12 = f32[4,786432]{1,0:T(4,128)S(1)} slice(f32[4,786944]{1,0:T(4,128)} %reshape.110), slice={[0:4], [511:786943]} | slice | bytes 25165824 | tf_op jit(solution)/shard_map/slice | solution.py:67
  150.9 0.0 collective-permute-done.2
  151.0 0.0 collective-permute-done.3
  151.0 0.0 copy-done.1
  151.0 0.0 copy-done.5
  151.0 11.5 %fusion.2 = f32[4,512,1536]{2,1,0:T(8,128)} fusion(f32[1,4,512,1536]{3,1,2,0:T(4,128)S(1)} %bitcast.44, pred[512,1536]{1,0:T(8,128)(4,1)S(1)} %fusion.10, f32[512,4,128]{2,0,1:T(8,128)S(1)} %copy-done.1, f32[4,128]{1,0:T(4,128)S(1)} %copy-done.5, bf16[512,512]{1,0:T(8,128)(2,1)S(1)} %convolution_convert_fusion.1, ...), kind=kOutput, calls=%fused_computation.3 | convolution fusion | flops 819986432 | bytes 28575744 | tf_op jit(solution)/shard_map/ihd,jhd->hij/dot_general | solution.py:102
  162.5 10.5 %fusion.23 = f32[4,512]{1,0:T(4,128)S(1)} fusion(f32[4,512,1536]{2,1,0:T(8,128)} %fusion.2), kind=kOutput, calls=%fused_computation.47 | output fusion | flops 6292991 | bytes 12591104 | tf_op jit(solution)/shard_map/sub | solution.py:110
  173.0 0.0 collective-permute-done
  173.0 0.0 collective-permute-done.1
  173.0 2.7 %pad_maximum_fusion = bf16[1536,512]{1,0:T(8,128)(2,1)} fusion(bf16[512,512]{1,0:T(8,128)(2,1)} %convolution_convert_fusion.3, bf16[512,512]{1,0:T(8,128)(2,1)} %collective-permute-done.1, bf16[512,512]{1,0:T(8,128)(2,1)} %collective-permute-done), kind=kLoop, calls=%fused_computation.23 | loop fusion | flops 4718592 | bytes 3145728 | tf_op jit(solution)/shard_map/concatenate | solution.py:92
  175.7 2.6 %copy.45 = bf16[1536,512]{0,1:T(8,128)(2,1)} copy(bf16[1536,512]{1,0:T(8,128)(2,1)} %pad_maximum_fusion) | data formatting | bytes 3145728 | tf_op jit(solution)/shard_map/reshape | solution.py:98
  178.3 10.9 %fusion.16 = bf16[4,128,512]{2,1,0:T(8,128)(2,1)S(1)} fusion(bf16[1536,4,128]{0,2,1:T(8,128)(2,1)} %bitcast.48, f32[4,512]{1,0:T(4,128)S(1)} %fusion.23, f32[4,512,1536]{2,1,0:T(8,128)} %fusion.2), kind=kOutput, calls=%fused_computation.28 | convolution fusion | flops 815009280 | bytes 14688256 | tf_op jit(solution)/shard_map/hij,jhd->ihd/dot_general | solution.py:111
  189.2 0.0 copy-done
  189.2 1.3 convolution_convert_fusion
  190.4 0.2 copy.58
  190.6 0.0 copy-start.2
  190.7 45.7 %all_to_all.16 = bf16[4,512,512]{2,1,0:T(8,128)(2,1)S(1)} all-to-all(bf16[4,512,512]{2,1,0:T(8,128)(2,1)S(1)} %bitcast.45), channel_id=1, replica_groups=mesh['seq'=64,'tp'=4] {'tp'}, dimensions={0} | all-to-all | bytes 4194304 | tf_op jit(solution)/shard_map/all_to_all | solution.py:37
  236.3 0.0 copy-start.6
  236.3 0.0 copy-start.7
  236.3 0.3 convert_reduce_fusion
  236.6 0.0 copy-done.2
  236.7 0.3 fusion.20
  237.0 18.4 %all_to_all.17 = f32[4,1,1024]{2,1,0:T(1,128)S(1)} all-to-all(f32[4,1,1024]{2,1,0:T(1,128)S(1)} %broadcast_in_dim.19), channel_id=1, replica_groups=mesh['seq'=64,'tp'=4] {'tp'}, dimensions={0} | all-to-all | bytes 32768 | tf_op jit(solution)/shard_map/all_to_all | solution.py:9
  255.4 0.0 copy-done.6
  255.4 0.0 copy-done.7
  255.5 2.1 add_convert_fusion
  (8 shorter events, 0.1 us)
Async XLA Ops:
  0.0 189.2 %copy-start = (bf16[512,2048]{1,0:T(8,128)(2,1)S(1)}, bf16[512,2048]{1,0:T(8,128)(2,1)}, u32[]{:S(2)}) copy-start(bf16[512,2048]{1,0:T(8,128)(2,1)} %param.15) | copy-start | bytes 6291460
  2.9 59.4 %all-to-all-start = ((bf16[4,512,512]{1,2,0:T(8,128)(2,1)}), bf16[4,512,512]{1,2,0:T(8,128)(2,1)}, u32[]{:S(2)}, u32[]{:S(2)}) async-start(bf16[4,512,512]{1,2,0:T(8,128)(2,1)} %broadcast_in_dim.12), calls=%async_computation | async-start | bytes 4194304 | tf_op jit(solution)/shard_map/all_to_all | solution.py:9
  11.9 23.3 %copy-start.8 = (bf16[2048,512]{1,0:T(8,128)(2,1)S(1)}, bf16[2048,512]{1,0:T(8,128)(2,1)}, u32[]{:S(2)}) copy-start(bf16[2048,512]{1,0:T(8,128)(2,1)} %param.14) | copy-start | bytes 6291460
  62.2 8.6 %copy-start.3 = (bf16[2048,512]{1,0:T(8,128)(2,1)S(1)}, bf16[2048,512]{1,0:T(8,128)(2,1)}, u32[]{:S(2)}) copy-start(bf16[2048,512]{1,0:T(8,128)(2,1)} %param.13) | copy-start | bytes 6291460
  65.9 15.5 %copy-start.9 = (bf16[2048,512]{1,0:T(8,128)(2,1)S(1)}, bf16[2048,512]{1,0:T(8,128)(2,1)}, u32[]{:S(2)}) copy-start(bf16[2048,512]{1,0:T(8,128)(2,1)} %param.11) | copy-start | bytes 6291460
  65.9 85.0 %collective-permute-start.2 = (bf16[512,512]{1,0:T(8,128)(2,1)S(1)}, bf16[512,512]{1,0:T(8,128)(2,1)}, u32[]{:S(2)}, u32[]{:S(2)}) collective-permute-start(bf16[512,512]{1,0:T(8,128)(2,1)S(1)} %convolution_convert_fusion.1), channel_id=1, source_target_pairs={{0,8},{4,12},{8,16},{12,20},{16,24},{20,28},{24,32},{28,36},{32,40... | collective-permute-start | bytes 1572872 | tf_op jit(solution)/shard_map/ppermute | solution.py:26
  68.9 82.0 %collective-permute-start.3 = (bf16[512,512]{1,0:T(8,128)(2,1)S(1)}, bf16[512,512]{1,0:T(8,128)(2,1)}, u32[]{:S(2)}, u32[]{:S(2)}) collective-permute-start(bf16[512,512]{1,0:T(8,128)(2,1)S(1)} %convolution_convert_fusion.1), channel_id=1, source_target_pairs={{0,4},{4,8},{8,12},{12,16},{16,20},{20,24},{24,28},{28,32},{32,36}... | collective-permute-start | bytes 1572872 | tf_op jit(solution)/shard_map/ppermute | solution.py:26
  74.5 12.7 %copy-start.4 = (f32[4,128]{1,0:T(4,128)S(1)}, f32[4,128]{1,0:T(4,128)}, u32[]{:S(2)}) copy-start(f32[4,128]{1,0:T(4,128)} %param.17) | copy-start | bytes 6148
  74.5 98.5 %collective-permute-start = (bf16[512,512]{1,0:T(8,128)(2,1)}, bf16[512,512]{1,0:T(8,128)(2,1)}, u32[]{:S(2)}, u32[]{:S(2)}) collective-permute-start(bf16[512,512]{1,0:T(8,128)(2,1)} %convolution_convert_fusion.3), channel_id=1, source_target_pairs={{0,8},{4,12},{8,16},{12,20},{16,24},{20,28},{24,32},{28,36},{32,40... | collective-permute-start | bytes 1572872 | tf_op jit(solution)/shard_map/ppermute | solution.py:26
  78.6 94.4 %collective-permute-start.1 = (bf16[512,512]{1,0:T(8,128)(2,1)}, bf16[512,512]{1,0:T(8,128)(2,1)}, u32[]{:S(2)}, u32[]{:S(2)}) collective-permute-start(bf16[512,512]{1,0:T(8,128)(2,1)} %convolution_convert_fusion.3), channel_id=1, source_target_pairs={{0,4},{4,8},{8,12},{12,16},{16,20},{20,24},{24,28},{28,32},{32,36}... | collective-permute-start | bytes 1572872 | tf_op jit(solution)/shard_map/ppermute | solution.py:26
  141.3 9.7 %copy-start.1 = (f32[512,4,128]{2,0,1:T(8,128)S(1)}, f32[512,4,128]{2,0,1:T(8,128)}, u32[]{:S(2)}) copy-start(f32[512,4,128]{2,0,1:T(8,128)} %copy.37) | copy-start | bytes 3145732
  141.3 9.7 %copy-start.5 = (f32[4,128]{1,0:T(4,128)S(1)}, f32[4,128]{1,0:T(4,128)}, u32[]{:S(2)}) copy-start(f32[4,128]{1,0:T(4,128)} %param.16) | copy-start | bytes 6148
  190.6 46.0 %copy-start.2 = (bf16[512,512]{1,0:T(8,128)(2,1)S(1)}, bf16[512,512]{1,0:T(8,128)(2,1)}, u32[]{:S(2)}) copy-start(bf16[512,512]{1,0:T(8,128)(2,1)} %param.10) | copy-start | bytes 1572868
  236.3 19.1 %copy-start.6 = (f32[512]{0:T(512)S(1)}, f32[512]{0:T(512)}, u32[]{:S(2)}) copy-start(f32[512]{0:T(512)} %param.19) | copy-start | bytes 6148
  236.3 19.1 %copy-start.7 = (f32[512]{0:T(512)S(1)}, f32[512]{0:T(512)}, u32[]{:S(2)}) copy-start(f32[512]{0:T(512)} %param.18) | copy-start | bytes 6148
where the time goes:
time: 258 us
  blocking collectives  64.1 us (25%)
  local copies, waits for them, and re-layouts  63.5 us (25%)
  matrix products  47.7 us (18%)
  other arithmetic  39.7 us (15%)
  waiting for transfers between devices  22.2 us (9%)
  starting transfers between devices  20.2 us (8%)
    all_to_all x1, blocking collectives, sent_and_summed(): lax.all_to_all(parts, axis, split_axis=0, concat_axis=0, tiled=True)  45.7 us
    another operation x1, other arithmetic  23.2 us
    all_to_all x1, waiting for transfers between devices, copy_for_each(): lax.all_to_all(jnp.broadcast_to(x[None], (peers, *x.shape)), axis, 0, 0,...  22.2 us
    unnamed x22, local copies, waits for them, and re-layouts  21.6 us
    all_to_all x1, blocking collectives, copy_for_each(): lax.all_to_all(jnp.broadcast_to(x[None], (peers, *x.shape)), axis, 0, 0,...  18.4 us
    reshape x1, local copies, waits for them, and re-layouts, shift_rows(): flat = padded.reshape(heads, seg * (span + 1))  15 us
    ppermute x4, starting transfers between devices, shifted(): return lax.ppermute(block, axis, route)  11.7 us
    dot_general x1, matrix products, shards(): jnp.einsum('ihd,jhd->hij', content_q, keys, preferred_element_type=jnp.fl...  11.5 us
  transfers between devices with their start and end apart: 5, of which 1 were waited for; matrix products, arithmetic and copies ran while one was open for 48% of the time, Pallas kernels for 0%

commit v1 on v0

v1 whole, which is shorter than its diff:
```python
import functools
import math

import jax
import jax.numpy as jnp
from jax import lax
from jax.experimental import pallas as pl
from jax.experimental.pallas import tpu as pltpu
from jax.sharding import PartitionSpec as P

MESH = pl.DeviceIdType.MESH
F32 = jnp.float32
BF16 = jnp.bfloat16
SEG = 512
ROWS = 128
CHUNKS = SEG // ROWS
HALF = ROWS // 2
WIDTH = 512
MODEL = 2048
HEAD = 128
FINE = 32
NEG = -1e30


def dot(a, b):
    return jnp.dot(a, b, preferred_element_type=F32)


def dot_t(a, b):
    return lax.dot_general(a, b, (((1,), (1,)), ((), ())), preferred_element_type=F32)


def copy_to(src, dst, sems, at, device):
    return pltpu.make_async_remote_copy(
        src_ref=src,
        dst_ref=dst,
        send_sem=sems[0].at[at],
        recv_sem=sems[1].at[at],
        device_id=device,
        device_id_type=MESH,
    )


def kernel(
    n_seq,
    hid, wq_in, wk_in, wv_in, wp_in, wo_in, bc, bp, gain, shift, out,
    g, wq, wkv, wp, wo, kv, cq, pq, rel, fine, coarse, att,
    opp, near_r, near_l, own, half_r, half_l, fin_r, fin_l, y, st_out, st_in,
    loc, up_s, up_r, dn_s, dn_r, y_s, y_r, d_s, d_r,
    or_s, or_r, ol_s, ol_r, fr_s, fr_r, fl_s, fl_r, st_s, st_r,
):
    s = lax.axis_index("seq")
    t = lax.axis_index("tp")
    core = lax.rem(s, 2)
    low = lax.rem(s // 2, 2)
    z = 2 * t + low
    right, left, across = lax.rem(t + 1, 4), lax.rem(t + 3, 4), lax.rem(t + 2, 4)
    mate = s + 2 - 4 * low
    up = (mate, lax.rem(t + low, 4))
    down = (mate, lax.rem(t + 3 + low, 4))
    twin = (s + 1 - 2 * core, t)
    to_right, to_left, to_across = (s, right), (s, left), (s, across)
    front = low == 0
    has_next = jnp.logical_and(front, s + 4 < n_seq)
    has_prev = jnp.logical_and(front, s >= 4)
    next_line = (lax.rem(s + 4, n_seq), t)
    prev_line = (lax.rem(s + n_seq - 4, n_seq), t)

    barrier = pltpu.get_barrier_semaphore()
    for device in (up, down, twin, to_right, to_left, to_across, next_line, prev_line):
        pl.semaphore_signal(barrier, inc=1, device_id=device, device_id_type=MESH)

    own_cols = pl.ds(pl.multiple_of(t * WIDTH, WIDTH), WIDTH)
    loads = [
        pltpu.make_async_copy(hid, g.at[low, :, own_cols], loc.at[0]),
        pltpu.make_async_copy(wp_in, wp, loc.at[1]),
        pltpu.make_async_copy(wk_in, wkv.at[:, pl.ds(0, WIDTH)], loc.at[2]),
        pltpu.make_async_copy(wv_in, wkv.at[:, pl.ds(WIDTH, WIDTH)], loc.at[3]),
        pltpu.make_async_copy(wq_in, wq, loc.at[4]),
    ]
    for c in range(4):
        loads.append(pltpu.make_async_copy(wo_in.at[:, pl.ds(c * WIDTH, WIDTH)], wo.at[c], loc.at[5 + c]))
    for load in loads:
        load.start()

    pl.semaphore_wait(barrier, 8)
    loads[0].wait()

    def block(z_from, r):
        cols = pl.ds(pl.multiple_of((z_from // 2) * WIDTH, WIDTH), WIDTH)
        return g.at[lax.rem(z_from, 2), pl.ds(r * ROWS, ROWS), cols]

    reach_up = [4 if r % 2 == 0 else 3 for r in range(CHUNKS)]
    reach_down = [7 - reach_up[r] for r in range(CHUNKS)]

    def send_up(r, d):
        ref = block(lax.rem(z + 8 - d, 8), r)
        return copy_to(ref, ref, (up_s, up_r), (d, r), up)

    def send_down(r, d):
        ref = block(lax.rem(z + d, 8), r)
        return copy_to(ref, ref, (dn_s, dn_r), (d, r), down)

    def came_up(r, d):
        ref = block(lax.rem(z + 8 - d, 8), r)
        return copy_to(ref, ref, (up_s, up_r), (d - 1, r), down)

    def came_down(r, d):
        ref = block(lax.rem(z + d, 8), r)
        return copy_to(ref, ref, (dn_s, dn_r), (d - 1, r), up)

    def tables():
        k = lax.broadcasted_iota(jnp.int32, (FINE, MODEL // 2), 1).astype(F32)
        freq = jnp.exp(k * (-math.log(10000.0) / (MODEL // 2)))
        row = lax.broadcasted_iota(jnp.int32, (FINE, MODEL // 2), 0)
        angle = (FINE - 1 - row).astype(F32) * freq
        fine[0] = jnp.sin(angle)
        fine[1] = jnp.cos(angle)
        n = 3 * SEG // FINE
        for part in range(n // 16):
            row = lax.broadcasted_iota(jnp.int32, (16, MODEL // 2), 0) + part * 16
            angle = (FINE * (n - 1 - row)).astype(F32) * freq[:16]
            coarse[0, part * 16 : part * 16 + 16, :] = jnp.sin(angle)
            coarse[1, part * 16 : part * 16 + 16, :] = jnp.cos(angle)

    def rel_rows(first, count):
        @pl.loop(first, first + count)
        def _(c):
            at = pl.multiple_of(c * 8, 8)
            sa, ca = coarse[0, pl.ds(at, 8), :], coarse[1, pl.ds(at, 8), :]
            sf, cf = fine[0], fine[1]
            sines, cosines = [], []
            for b in range(8):
                sb, cb = sa[b : b + 1], ca[b : b + 1]
                sines.append((sb * cf + cb * sf).astype(BF16))
                cosines.append((cb * cf - sb * sf).astype(BF16))
            half = MODEL // 2
            total = dot(jnp.concatenate(sines, 0), wp[:half]) + dot(jnp.concatenate(cosines, 0), wp[half:])
            rel[pl.ds(pl.multiple_of(c * 256, 256), 256), :] = total.astype(BF16)

    other_slot = jnp.where(front, 3, 0)

    def kv_rows(slot, r):
        return pl.ds(pl.multiple_of(slot * SEG + r * ROWS, ROWS), ROWS)

    def shift_line(r):
        return copy_to(kv.at[kv_rows(3, r)], kv.at[kv_rows(0, r)], (y_s, y_r), r, next_line)

    def shift_line_in(r):
        return copy_to(kv.at[kv_rows(3, r)], kv.at[kv_rows(0, r)], (y_s, y_r), r, prev_line)

    def to_twin(slot, r):
        return copy_to(kv.at[kv_rows(slot, r)], kv.at[kv_rows(1, r)], (d_s, d_r), r, twin)

    def project(r):
        rows = pl.ds(r * ROWS, ROWS)
        mine = g[low, rows, :]
        both = jnp.concatenate([mine, g[1 - low, rows, :]], 0)
        made = dot(both, wkv[...]).astype(BF16)
        kv[kv_rows(2, r), :] = made[:ROWS]
        kv[kv_rows(other_slot, r), :] = made[ROWS:]

        @pl.when(has_next)
        def _():
            shift_line(r).start()

        @pl.when(core == 0)
        def _():
            to_twin(2, r).start()

        @pl.when(jnp.logical_and(core == 1, low == 1))
        def _():
            to_twin(0, r).start()

        q = dot(mine, wq[...]).astype(BF16).astype(F32)
        for h in range(4):
            cols = slice(h * HEAD, (h + 1) * HEAD)
            cq[r * ROWS : (r + 1) * ROWS, cols] = (q[:, cols] + bc[h : h + 1, :]).astype(BF16)
            pq[r * ROWS : (r + 1) * ROWS, cols] = (q[:, cols] + bp[h : h + 1, :]).astype(BF16)

    @pl.when(jnp.logical_and(front, s < 4))
    def _():
        kv[0:SEG, :] = jnp.zeros((SEG, 2 * WIDTH), BF16)

    rel[3 * SEG :, :] = jnp.zeros((ROWS, WIDTH), BF16)

    side = {0: tables, 1: lambda: (loads[1].wait(), rel_rows(0, 2)), 3: lambda: rel_rows(2, 2), 5: lambda: rel_rows(4, 2)}
    last = CHUNKS - 1 + 2 * 4
    for key in range(last + 1):
        for d in range(5):
            r = key - 2 * d
            if r < 0 or r >= CHUNKS:
                continue
            if d == 0:
                send_up(r, 0).start()
                send_down(r, 0).start()
                continue
            if d <= reach_up[r]:
                came_up(r, d).wait_recv()
                if d < reach_up[r]:
                    send_up(r, d).start()
            if d <= reach_down[r]:
                came_down(r, d).wait_recv()
                if d < reach_down[r]:
                    send_down(r, d).start()
        if key in side:
            side[key]()
        if key >= 8:
            if key == 8:
                for load in loads[2:5]:
                    load.wait()
            project(key - 8)

    for r in range(CHUNKS):
        @pl.when(has_prev)
        def _():
            shift_line_in(r).wait_recv()

        @pl.when(jnp.logical_and(core == 1, front))
        def _():
            to_twin(0, r).start()

    for r in range(CHUNKS):
        to_twin(0, r).wait_recv()
    for load in loads[5:]:
        load.wait()

    start = jnp.maximum(2 * SEG - SEG * s, 0)
    scale = math.log2(math.e) / math.sqrt(HEAD)

    def attend(r):
        i0 = r * ROWS
        keys = 2 * SEG + ROWS + i0
        span = keys + ROWS
        e0 = SEG - ROWS - i0
        outside = jnp.where(lax.broadcasted_iota(jnp.int32, (1, keys), 1) >= start, 0.0, NEG).astype(F32)
        causal = lax.broadcasted_iota(jnp.int32, (ROWS, ROWS), 1) <= lax.broadcasted_iota(jnp.int32, (ROWS, ROWS), 0)

        def one(h):
            cols = pl.ds(pl.multiple_of(h * HEAD, HEAD), HEAD)
            vcols = pl.ds(pl.multiple_of(WIDTH + h * HEAD, HEAD), HEAD)
            content = dot_t(cq[i0 : i0 + ROWS, cols], kv[0:keys, cols])
            position = dot_t(pq[i0 : i0 + ROWS, cols], rel[e0 : e0 + span, cols])
            position = pltpu.roll(position, span - (ROWS - 1), 1, stride=1, stride_axis=0)[:, :keys]
            score = content + position + outside
            tail = jnp.where(causal, score[:, keys - ROWS :], NEG)
            score = jnp.concatenate([score[:, : keys - ROWS], tail], 1)
            top = jnp.max(score, axis=1, keepdims=True)
            e = jnp.exp2((score - top) * scale)
            norm = 1.0 / jnp.sum(e, axis=1, keepdims=True)
            att[i0 : i0 + ROWS, cols] = dot((e * norm).astype(BF16), kv[0:keys, vcols]).astype(BF16)

        @pl.loop(0, 2)
        def _(pair):
            one(2 * pair)
            one(2 * pair + 1)

    def opp_right(r):
        return copy_to(opp.at[r, pl.ds(0, HALF)], half_r.at[r], (or_s, or_r), r, to_right)

    def opp_left(r):
        return copy_to(opp.at[r, pl.ds(HALF, HALF)], half_l.at[r], (ol_s, ol_r), r, to_left)

    def fin_right(r):
        return copy_to(near_r.at[r], fin_r.at[r], (fr_s, fr_r), r, to_right)

    def fin_left(r):
        return copy_to(near_l.at[r], fin_l.at[r], (fl_s, fl_r), r, to_left)

    def output(r):
        a = att[r * ROWS : (r + 1) * ROWS, :]
        opp[r] = dot(a, wo[across]).astype(BF16)
        opp_right(r).start()
        opp_left(r).start()
        near_r[r] = dot(a, wo[right]).astype(BF16)
        near_l[r] = dot(a, wo[left]).astype(BF16)
        own[r] = dot(a, wo[t]).astype(BF16)

    def pass_on(r):
        opp_right(r).wait_recv()
        near_r[r, :HALF, :] = (near_r[r, :HALF, :].astype(F32) + half_r[r].astype(F32)).astype(BF16)
        fin_right(r).start()
        opp_left(r).wait_recv()
        near_l[r, HALF:, :] = (near_l[r, HALF:, :].astype(F32) + half_l[r].astype(F32)).astype(BF16)
        fin_left(r).start()

    others = (to_right, to_across, to_left)

    def stats_to(i, r):
        return copy_to(st_out.at[r], st_in.at[i, r], (st_s, st_r), (i, r), others[i])

    def collect(r):
        fin_right(r).wait_recv()
        fin_left(r).wait_recv()
        rows = pl.ds(r * ROWS, ROWS)
        total = g[low, rows, own_cols].astype(F32) + (
            own[r].astype(F32) + fin_r[r].astype(F32) + fin_l[r].astype(F32)
        )
        y[r] = total
        mean = jnp.sum(total, axis=1, keepdims=True) * (1.0 / WIDTH)
        centred = total - mean
        square = jnp.sum(centred * centred, axis=1, keepdims=True)
        lane = lax.broadcasted_iota(jnp.int32, (ROWS, 128), 1)
        both = jnp.where(lane == 0, mean, jnp.where(lane == 1, square, 0.0))
        st_out[r] = both.T[:8, :]
        for i in range(3):
            stats_to(i, r).start()

    def finish(r):
        for i in range(3):
            stats_to(i, r).wait_recv()
        stack = jnp.concatenate(
            [st_out[r], st_in[0, r], st_in[1, r], st_in[2, r], jnp.zeros((96, 128), F32)], 0
        ).T
        means = [stack[:, 8 * i : 8 * i + 1] for i in range(4)]
        squares = [stack[:, 8 * i + 1 : 8 * i + 2] for i in range(4)]
        mean = (means[0] + means[1] + means[2] + means[3]) * 0.25
        square = squares[0] + squares[1] + squares[2] + squares[3]
        for m in means:
            square = square + WIDTH * ((m - mean) * (m - mean))
        factor = lax.rsqrt(square * (1.0 / MODEL) + 1e-05)
        normed = (y[r] - mean) * factor
        out[r * ROWS : (r + 1) * ROWS, :] = (normed * gain[...] + shift[...]).astype(BF16)

    for r in range(CHUNKS):
        attend(r)
        output(r)
        if r >= 1:
            pass_on(r - 1)
        if r >= 2:
            collect(r - 2)
    pass_on(CHUNKS - 1)
    collect(CHUNKS - 2)
    for r in range(CHUNKS - 1):
        finish(r)
    collect(CHUNKS - 1)
    finish(CHUNKS - 1)

    for r in range(CHUNKS):
        for d in range(4):
            if d < reach_up[r]:
                send_up(r, d).wait_send()
            if d < reach_down[r]:
                send_down(r, d).wait_send()

        @pl.when(has_next)
        def _():
            shift_line(r).wait_send()

        to_twin(0, r).wait_send()
        for copy in (opp_right(r), opp_left(r), fin_right(r), fin_left(r)):
            copy.wait_send()
        for i in range(3):
            stats_to(i, r).wait_send()


def layer(n_seq, hidden_in, w_query, w_key, w_value, w_pos, w_out, bias_content, bias_pos, norm_gain, norm_bias):
    anywhere = pl.BlockSpec(memory_space=pl.ANY)
    vmem = pl.BlockSpec(memory_space=pltpu.VMEM)
    dma = pltpu.SemaphoreType.DMA
    per_chunk = [dma((CHUNKS,))] * 2
    return pl.pallas_call(
        functools.partial(kernel, n_seq),
        out_shape=jax.ShapeDtypeStruct((SEG, WIDTH), BF16),
        in_specs=[anywhere] * 6 + [vmem] * 4,
        out_specs=vmem,
        scratch_shapes=[
            pltpu.VMEM((2, SEG, MODEL), BF16),
            pltpu.VMEM((MODEL, WIDTH), BF16),
            pltpu.VMEM((MODEL, 2 * WIDTH), BF16),
            pltpu.VMEM((MODEL, WIDTH), BF16),
            pltpu.VMEM((4, WIDTH, WIDTH), BF16),
            pltpu.VMEM((4 * SEG, 2 * WIDTH), BF16),
            pltpu.VMEM((SEG, WIDTH), BF16),
            pltpu.VMEM((SEG, WIDTH), BF16),
            pltpu.VMEM((3 * SEG + ROWS, WIDTH), BF16),
            pltpu.VMEM((2, FINE, MODEL // 2), F32),
            pltpu.VMEM((2, 3 * SEG // FINE, MODEL // 2), F32),
            pltpu.VMEM((SEG, WIDTH), BF16),
            pltpu.VMEM((CHUNKS, ROWS, WIDTH), BF16),
            pltpu.VMEM((CHUNKS, ROWS, WIDTH), BF16),
            pltpu.VMEM((CHUNKS, ROWS, WIDTH), BF16),
            pltpu.VMEM((CHUNKS, ROWS, WIDTH), BF16),
            pltpu.VMEM((CHUNKS, HALF, WIDTH), BF16),
            pltpu.VMEM((CHUNKS, HALF, WIDTH), BF16),
            pltpu.VMEM((CHUNKS, ROWS, WIDTH), BF16),
            pltpu.VMEM((CHUNKS, ROWS, WIDTH), BF16),
            pltpu.VMEM((CHUNKS, ROWS, WIDTH), F32),
            pltpu.VMEM((CHUNKS, 8, 128), F32),
            pltpu.VMEM((3, CHUNKS, 8, 128), F32),
            dma((9,)),
            dma((4, CHUNKS)), dma((4, CHUNKS)), dma((4, CHUNKS)), dma((4, CHUNKS)),
            *per_chunk, *per_chunk, *per_chunk, *per_chunk, *per_chunk, *per_chunk,
            dma((3, CHUNKS)), dma((3, CHUNKS)),
        ],
        compiler_params=pltpu.CompilerParams(
            collective_id=0, has_side_effects=True, vmem_limit_bytes=60 * 2**20
        ),
    )(
        hidden_in, w_query, w_key, w_value, w_pos, w_out, bias_content, bias_pos,
        norm_gain.reshape(1, WIDTH), norm_bias.reshape(1, WIDTH),
    )


def solution(mesh):
    in_specs = (
        P("seq", "tp"),
        P(None, "tp"),
        P(None, "tp"),
        P(None, "tp"),
        P(None, "tp"),
        P("tp", None),
        P("tp", None),
        P("tp", None),
        P("tp"),
        P("tp"),
    )
    return jax.shard_map(
        functools.partial(layer, mesh.shape["seq"]),
        mesh=mesh,
        in_specs=in_specs,
        out_specs=P("seq", "tp"),
        check_vma=False,
    )
```

time: 258 us -> 116 us (0.45)
  Pallas kernels: 0 us -> 114 us
  blocking collectives: 64.1 us -> 0 us
  local copies, waits for them, and re-layouts: 63.5 us -> 1.87 us
  matrix products: 47.7 us -> 0 us
  other arithmetic: 39.7 us -> 0 us
  waiting for transfers between devices: 22.2 us -> 0 us
  starting transfers between devices: 20.2 us -> 0 us
    pallas_call x0 -> x1, Pallas kernels: none -> 114 us  [layer(): pl.pallas_call(functools.partial(kernel, n_seq), out_shape=jax.ShapeDtype...]
    all_to_all x2 -> x0, blocking collectives: 64.1 us -> none  [the longest x1 45.7 us: sent_and_summed(): lax.all_to_all(parts, axis, split_axis=0, concat_axis=0, tiled=True)]
    dot_general x8 -> x0, matrix products: 47.7 us -> none  [the longest x1 11.5 us: shards(): jnp.einsum('ihd,jhd->hij', content_q, keys, preferred_element_type=jnp.fl...]
    another operation x1 -> x0, other arithmetic: 23.2 us -> none
    all_to_all x1 -> x0, waiting for transfers between devices: 22.2 us -> none  [copy_for_each(): lax.all_to_all(jnp.broadcast_to(x[None], (peers, *x.shape)), axis, 0, 0,...]
    reshape x4 -> x0, local copies, waits for them, and re-layouts: 20 us -> none  [the longest x1 15 us: shift_rows(): flat = padded.reshape(heads, seg * (span + 1))]
    unnamed x22 -> x1, local copies, waits for them, and re-layouts: 21.6 us -> 1.87 us
    ppermute x4 -> x0, starting transfers between devices: 11.7 us -> none  [shifted(): return lax.ppermute(block, axis, route)]
  transfers between devices with their start and end apart: 5 -> 0, of which waited for: 1 -> 0; matrix products, arithmetic and copies ran while one was open for 48% -> 0% of each run, Pallas kernels for 0% -> 0%
where the time goes in v1:
time: 116 us; the launch traced here: 115 us
  Pallas kernels  114 us (98%)
  local copies, waits for them, and re-layouts  1.87 us (2%)
    pallas_call x1, Pallas kernels, layer(): pl.pallas_call(functools.partial(kernel, n_seq), out_shape=jax.ShapeDtype...  114 us

profile of v1, /device:TPU:6, one launch (start us, length us, event | category | flops | bytes accessed | tf_op | source)
XLA Modules:
  0.0 115.5 jit_solution(1165414784967447139)
XLA Ops:
  0.0 113.6 %shard_map.100 = bf16[512,512]{1,0:T(8,128)(2,1)} custom-call(bf16[512,512]{1,0:T(8,128)(2,1)} %hid.1, bf16[2048,512]{1,0:T(8,128)(2,1)} %wq_in.1, bf16[2048,512]{1,0:T(8,128)(2,1)} %wk_in.1, bf16[2048,512]{1,0:T(8,128)(2,1)} %wv_in.1, bf16[2048,512]{1,0:T(8,128)(2,1)} %wp_in.1, bf16[512,2048]{1,0:T(8,128)(2,1)} %wo_in.1, f32[4,128]{1,0:T(4,128)} %bc.1, ...), custom_call_target="tpu_custom_call" | custom-call | tf_op jit(solution)/shard_map/pallas_call | solution.py:362
  113.6 1.9 %copy.12 = bf16[512,512]{1,0:T(8,128)(2,1)} copy(bf16[512,512]{1,0:T(8,128)(2,1)} %shard_map.100) | data formatting | bytes 1048576

commit v2 on v1

--- a/solution.py
+++ b/solution.py
@@ -15,6 +15,8 @@
 ROWS = 128
 CHUNKS = SEG // ROWS
 HALF = ROWS // 2
+PIECE = 64
+PIECES = SEG // PIECE
 WIDTH = 512
 MODEL = 2048
 HEAD = 128
@@ -39,6 +41,31 @@
         device_id=device,
         device_id_type=MESH,
     )
+
+
+def gather_order(slot=1.4, latency=3.6, weight=0.5):
+    events = []
+    done = [0.0] * PIECES
+    for way, reach in enumerate(REACH):
+        clock, ends = 0.0, {}
+        left = [(p, d) for p in range(PIECES) for d in range(reach[p])]
+        while left:
+            ready = {(p, d): 0.0 if d == 0 else ends[p, d - 1] + latency for p, d in left if d == 0 or (p, d - 1) in ends}
+            clock = max(clock, min(ready.values()))
+            pick = min((x for x in ready if ready[x] <= clock + 1e-9), key=lambda x: (weight * x[0] - reach[x[0]] + x[1], x[0]))
+            left.remove(pick)
+            events.append((clock, way, *pick))
+            clock += slot
+            ends[pick] = clock
+        for p in range(PIECES):
+            done[p] = max(done[p], ends[p, reach[p] - 1] + latency)
+    for c in range(CHUNKS):
+        per = ROWS // PIECE
+        events.append((max(done[c * per : (c + 1) * per]), 2, c, 0))
+    return sorted(events)
+
+
+REACH = ([4 if p % 2 == 0 else 3 for p in range(PIECES)], [3 if p % 2 == 0 else 4 for p in range(PIECES)])
 
 
 def kernel(
@@ -83,31 +110,17 @@
     for load in loads:
         load.start()
 
-    pl.semaphore_wait(barrier, 8)
-    loads[0].wait()
-
-    def block(z_from, r):
+    def block(z_from, p):
         cols = pl.ds(pl.multiple_of((z_from // 2) * WIDTH, WIDTH), WIDTH)
-        return g.at[lax.rem(z_from, 2), pl.ds(r * ROWS, ROWS), cols]
-
-    reach_up = [4 if r % 2 == 0 else 3 for r in range(CHUNKS)]
-    reach_down = [7 - reach_up[r] for r in range(CHUNKS)]
-
-    def send_up(r, d):
-        ref = block(lax.rem(z + 8 - d, 8), r)
-        return copy_to(ref, ref, (up_s, up_r), (d, r), up)
-
-    def send_down(r, d):
-        ref = block(lax.rem(z + d, 8), r)
-        return copy_to(ref, ref, (dn_s, dn_r), (d, r), down)
-
-    def came_up(r, d):
-        ref = block(lax.rem(z + 8 - d, 8), r)
-        return copy_to(ref, ref, (up_s, up_r), (d - 1, r), down)
-
-    def came_down(r, d):
-        ref = block(lax.rem(z + d, 8), r)
-        return copy_to(ref, ref, (dn_s, dn_r), (d - 1, r), up)
+        return g.at[lax.rem(z_from, 2), pl.ds(p * PIECE, PIECE), cols]
+
+    def send(way, p, d):
+        ref = block(lax.rem(z + d, 8) if way else lax.rem(z + 8 - d, 8), p)
+        return copy_to(ref, ref, (dn_s, dn_r) if way else (up_s, up_r), (d, p), down if way else up)
+
+    def came(way, p, d):
+        ref = block(lax.rem(z + d, 8) if way else lax.rem(z + 8 - d, 8), p)
+        return copy_to(ref, ref, (dn_s, dn_r) if way else (up_s, up_r), (d - 1, p), up if way else down)
 
     def tables():
         k = lax.broadcasted_iota(jnp.int32, (FINE, MODEL // 2), 1).astype(F32)
@@ -123,20 +136,17 @@
             coarse[0, part * 16 : part * 16 + 16, :] = jnp.sin(angle)
             coarse[1, part * 16 : part * 16 + 16, :] = jnp.cos(angle)
 
-    def rel_rows(first, count):
-        @pl.loop(first, first + count)
-        def _(c):
-            at = pl.multiple_of(c * 8, 8)
-            sa, ca = coarse[0, pl.ds(at, 8), :], coarse[1, pl.ds(at, 8), :]
-            sf, cf = fine[0], fine[1]
-            sines, cosines = [], []
-            for b in range(8):
-                sb, cb = sa[b : b + 1], ca[b : b + 1]
-                sines.append((sb * cf + cb * sf).astype(BF16))
-                cosines.append((cb * cf - sb * sf).astype(BF16))
-            half = MODEL // 2
-            total = dot(jnp.concatenate(sines, 0), wp[:half]) + dot(jnp.concatenate(cosines, 0), wp[half:])
-            rel[pl.ds(pl.multiple_of(c * 256, 256), 256), :] = total.astype(BF16)
+    def rel_rows(c):
+        sa, ca = coarse[0, c * 8 : c * 8 + 8, :], coarse[1, c * 8 : c * 8 + 8, :]
+        sf, cf = fine[0], fine[1]
+        sines, cosines = [], []
+        for b in range(8):
+            sb, cb = sa[b : b + 1], ca[b : b + 1]
+            sines.append((sb * cf + cb * sf).astype(BF16))
+            cosines.append((cb * cf - sb * sf).astype(BF16))
+        half = MODEL // 2
+        total = dot(jnp.concatenate(sines, 0), wp[:half]) + dot(jnp.concatenate(cosines, 0), wp[half:])
+        rel[c * 256 : (c + 1) * 256, :] = total.astype(BF16)
 
     other_slot = jnp.where(front, 3, 0)
 
@@ -184,32 +194,32 @@
 
     rel[3 * SEG :, :] = jnp.zeros((ROWS, WIDTH), BF16)
 
-    side = {0: tables, 1: lambda: (loads[1].wait(), rel_rows(0, 2)), 3: lambda: rel_rows(2, 2), 5: lambda: rel_rows(4, 2)}
-    last = CHUNKS - 1 + 2 * 4
-    for key in range(last + 1):
-        for d in range(5):
-            r = key - 2 * d
-            if r < 0 or r >= CHUNKS:
-                continue
-            if d == 0:
-                send_up(r, 0).start()
-                send_down(r, 0).start()
-                continue
-            if d <= reach_up[r]:
-                came_up(r, d).wait_recv()
-                if d < reach_up[r]:
-                    send_up(r, d).start()
-            if d <= reach_down[r]:
-                came_down(r, d).wait_recv()
-                if d < reach_down[r]:
-                    send_down(r, d).start()
-        if key in side:
-            side[key]()
-        if key >= 8:
-            if key == 8:
-                for load in loads[2:5]:
-                    load.wait()
-            project(key - 8)
+    tables()
+    loads[0].wait()
+    pl.semaphore_wait(barrier, 8)
+
+    projected = False
+    passed, made = 0, 0
+    for _, way, p, d in gather_order():
+        if way < 2:
+            if d > 0:
+                came(way, p, d).wait_recv()
+            send(way, p, d).start()
+            passed += 1
+            if passed % 4 == 2 and passed > 4 and made < 6:
+                if made == 0:
+                    loads[1].wait()
+                rel_rows(made)
+                made += 1
+            continue
+        if not projected:
+            for load in loads[2:5]:
+                load.wait()
+            projected = True
+        for piece in range(p * ROWS // PIECE, (p + 1) * ROWS // PIECE):
+            came(0, piece, REACH[0][piece]).wait_recv()
+            came(1, piece, REACH[1][piece]).wait_recv()
+        project(p)
 
     for r in range(CHUNKS):
         @pl.when(has_prev)
@@ -237,8 +247,8 @@
         causal = lax.broadcasted_iota(jnp.int32, (ROWS, ROWS), 1) <= lax.broadcasted_iota(jnp.int32, (ROWS, ROWS), 0)
 
         def one(h):
-            cols = pl.ds(pl.multiple_of(h * HEAD, HEAD), HEAD)
-            vcols = pl.ds(pl.multiple_of(WIDTH + h * HEAD, HEAD), HEAD)
+            cols = slice(h * HEAD, (h + 1) * HEAD)
+            vcols = slice(WIDTH + h * HEAD, WIDTH + (h + 1) * HEAD)
             content = dot_t(cq[i0 : i0 + ROWS, cols], kv[0:keys, cols])
             position = dot_t(pq[i0 : i0 + ROWS, cols], rel[e0 : e0 + span, cols])
             position = pltpu.roll(position, span - (ROWS - 1), 1, stride=1, stride_axis=0)[:, :keys]
@@ -250,10 +260,8 @@
             norm = 1.0 / jnp.sum(e, axis=1, keepdims=True)
             att[i0 : i0 + ROWS, cols] = dot((e * norm).astype(BF16), kv[0:keys, vcols]).astype(BF16)
 
-        @pl.loop(0, 2)
-        def _(pair):
-            one(2 * pair)
-            one(2 * pair + 1)
+        for h in range(4):
+            one(h)
 
     def opp_right(r):
         return copy_to(opp.at[r, pl.ds(0, HALF)], half_r.at[r], (or_s, or_r), r, to_right)
@@ -261,11 +269,13 @@
     def opp_left(r):
         return copy_to(opp.at[r, pl.ds(HALF, HALF)], half_l.at[r], (ol_s, ol_r), r, to_left)
 
-    def fin_right(r):
-        return copy_to(near_r.at[r], fin_r.at[r], (fr_s, fr_r), r, to_right)
-
-    def fin_left(r):
-        return copy_to(near_l.at[r], fin_l.at[r], (fl_s, fl_r), r, to_left)
+    def fin_right(r, i):
+        rows = pl.ds((1 - i) * HALF, HALF)
+        return copy_to(near_r.at[r, rows], fin_r.at[r, rows], (fr_s, fr_r), (i, r), to_right)
+
+    def fin_left(r, i):
+        rows = pl.ds(i * HALF, HALF)
+        return copy_to(near_l.at[r, rows], fin_l.at[r, rows], (fl_s, fl_r), (i, r), to_left)
 
     def output(r):
         a = att[r * ROWS : (r + 1) * ROWS, :]
@@ -273,16 +283,18 @@
         opp_right(r).start()
         opp_left(r).start()
         near_r[r] = dot(a, wo[right]).astype(BF16)
+        fin_right(r, 0).start()
         near_l[r] = dot(a, wo[left]).astype(BF16)
+        fin_left(r, 0).start()
         own[r] = dot(a, wo[t]).astype(BF16)
 
     def pass_on(r):
         opp_right(r).wait_recv()
         near_r[r, :HALF, :] = (near_r[r, :HALF, :].astype(F32) + half_r[r].astype(F32)).astype(BF16)
-        fin_right(r).start()
+        fin_right(r, 1).start()
         opp_left(r).wait_recv()
         near_l[r, HALF:, :] = (near_l[r, HALF:, :].astype(F32) + half_l[r].astype(F32)).astype(BF16)
-        fin_left(r).start()
+        fin_left(r, 1).start()
 
     others = (to_right, to_across, to_left)
 
@@ -290,8 +302,9 @@
         return copy_to(st_out.at[r], st_in.at[i, r], (st_s, st_r), (i, r), others[i])
 
     def collect(r):
-        fin_right(r).wait_recv()
-        fin_left(r).wait_recv()
+        for i in range(2):
+            fin_right(r, i).wait_recv()
+            fin_left(r, i).wait_recv()
         rows = pl.ds(r * ROWS, ROWS)
         total = g[low, rows, own_cols].astype(F32) + (
             own[r].astype(F32) + fin_r[r].astype(F32) + fin_l[r].astype(F32)
@@ -336,19 +349,17 @@
     collect(CHUNKS - 1)
     finish(CHUNKS - 1)
 
+    for way in range(2):
+        for p in range(PIECES):
+            for d in range(REACH[way][p]):
+                send(way, p, d).wait_send()
     for r in range(CHUNKS):
-        for d in range(4):
-            if d < reach_up[r]:
-                send_up(r, d).wait_send()
-            if d < reach_down[r]:
-                send_down(r, d).wait_send()
-
         @pl.when(has_next)
         def _():
             shift_line(r).wait_send()
 
         to_twin(0, r).wait_send()
-        for copy in (opp_right(r), opp_left(r), fin_right(r), fin_left(r)):
+        for copy in (opp_right(r), opp_left(r), fin_right(r, 0), fin_left(r, 0), fin_right(r, 1), fin_left(r, 1)):
             copy.wait_send()
         for i in range(3):
             stats_to(i, r).wait_send()
@@ -389,8 +400,9 @@
             pltpu.VMEM((CHUNKS, 8, 128), F32),
             pltpu.VMEM((3, CHUNKS, 8, 128), F32),
             dma((9,)),
-            dma((4, CHUNKS)), dma((4, CHUNKS)), dma((4, CHUNKS)), dma((4, CHUNKS)),
-            *per_chunk, *per_chunk, *per_chunk, *per_chunk, *per_chunk, *per_chunk,
+            dma((4, PIECES)), dma((4, PIECES)), dma((4, PIECES)), dma((4, PIECES)),
+            *per_chunk, *per_chunk, *per_chunk, *per_chunk,
+            dma((2, CHUNKS)), dma((2, CHUNKS)), dma((2, CHUNKS)), dma((2, CHUNKS)),
             dma((3, CHUNKS)), dma((3, CHUNKS)),
         ],
         compiler_params=pltpu.CompilerParams(

time: 116 us -> 111 us (0.957)
  Pallas kernels: 114 us -> 109 us
    pallas_call x1, Pallas kernels: 114 us -> 109 us  [layer(): pl.pallas_call(functools.partial(kernel, n_seq), out_shape=jax.ShapeDtype...]
where the time goes in v2:
time: 111 us
  Pallas kernels  109 us (98%)
  local copies, waits for them, and re-layouts  1.87 us (2%)
    pallas_call x1, Pallas kernels, layer(): pl.pallas_call(functools.partial(kernel, n_seq), out_shape=jax.ShapeDtype...  109 us

profile of v2, /device:TPU:6, one launch (start us, length us, event | category | flops | bytes accessed | tf_op | source)
XLA Modules:
  0.0 110.6 jit_solution(735904663427960086)
XLA Ops:
  0.0 108.7 %shard_map.100 = bf16[512,512]{1,0:T(8,128)(2,1)} custom-call(bf16[512,512]{1,0:T(8,128)(2,1)} %hid.1, bf16[2048,512]{1,0:T(8,128)(2,1)} %wq_in.1, bf16[2048,512]{1,0:T(8,128)(2,1)} %wk_in.1, bf16[2048,512]{1,0:T(8,128)(2,1)} %wv_in.1, bf16[2048,512]{1,0:T(8,128)(2,1)} %wp_in.1, bf16[512,2048]{1,0:T(8,128)(2,1)} %wo_in.1, f32[4,128]{1,0:T(4,128)} %bc.1, ...), custom_call_target="tpu_custom_call" | custom-call | tf_op jit(solution)/shard_map/pallas_call | solution.py:373
  108.7 1.9 %copy.12 = bf16[512,512]{1,0:T(8,128)(2,1)} copy(bf16[512,512]{1,0:T(8,128)(2,1)} %shard_map.100) | data formatting | bytes 1048576

commit v3 on v2

--- a/solution.py
+++ b/solution.py
@@ -194,7 +194,6 @@
 
     rel[3 * SEG :, :] = jnp.zeros((ROWS, WIDTH), BF16)
 
-    tables()
     loads[0].wait()
     pl.semaphore_wait(barrier, 8)
 
@@ -206,7 +205,9 @@
                 came(way, p, d).wait_recv()
             send(way, p, d).start()
             passed += 1
-            if passed % 4 == 2 and passed > 4 and made < 6:
+            if passed == 6:
+                tables()
+            if passed % 4 == 2 and passed > 8 and made < 6:
                 if made == 0:
                     loads[1].wait()
                 rel_rows(made)
@@ -372,7 +373,7 @@
     per_chunk = [dma((CHUNKS,))] * 2
     return pl.pallas_call(
         functools.partial(kernel, n_seq),
-        out_shape=jax.ShapeDtypeStruct((SEG, WIDTH), BF16),
+        out_shape=pltpu.VMEM((SEG, WIDTH), BF16),
         in_specs=[anywhere] * 6 + [vmem] * 4,
         out_specs=vmem,
         scratch_shapes=[
@@ -406,7 +407,7 @@
             dma((3, CHUNKS)), dma((3, CHUNKS)),
         ],
         compiler_params=pltpu.CompilerParams(
-            collective_id=0, has_side_effects=True, vmem_limit_bytes=60 * 2**20
+            collective_id=0, has_side_effects=True, vmem_limit_bytes=66_200_000
         ),
     )(
         hidden_in, w_query, w_key, w_value, w_pos, w_out, bias_content, bias_pos,

time: 111 us -> 109 us (0.982)
  no operation moved by 1% of the time
where the time goes in v3:
time: 109 us
  Pallas kernels  109 us (100%)
    pallas_call x1, Pallas kernels, layer(): pl.pallas_call(functools.partial(kernel, n_seq), out_shape=pltpu.VMEM((SE...  109 us

profile of v3, /device:TPU:6, one launch (start us, length us, event | category | flops | bytes accessed | tf_op | source)
XLA Modules:
  0.0 109.4 jit_solution(16762018202293596306)
XLA Ops:
  0.0 108.6 %shard_map.100 = bf16[512,512]{1,0:T(8,128)(2,1)S(1)} custom-call(bf16[512,512]{1,0:T(8,128)(2,1)} %hid.1, bf16[2048,512]{1,0:T(8,128)(2,1)} %wq_in.1, bf16[2048,512]{1,0:T(8,128)(2,1)} %wk_in.1, bf16[2048,512]{1,0:T(8,128)(2,1)} %wv_in.1, bf16[2048,512]{1,0:T(8,128)(2,1)} %wp_in.1, bf16[512,2048]{1,0:T(8,128)(2,1)} %wo_in.1, f32[4,128]{1,0:T(4,128)} %bc.1, ...), custom_call_target="tpu_custom_call" | custom-call | tf_op jit(solution)/shard_map/pallas_call | solution.py:374
  108.6 0.8 copy.12

commit v4 on v3

--- a/solution.py
+++ b/solution.py
@@ -43,7 +43,7 @@
     )
 
 
-def gather_order(slot=1.4, latency=3.6, weight=0.5):
+def gather_order(slot=1.4, latency=3.0, weight=0.34):
     events = []
     done = [0.0] * PIECES
     for way, reach in enumerate(REACH):
@@ -341,13 +341,12 @@
         output(r)
         if r >= 1:
             pass_on(r - 1)
-        if r >= 2:
-            collect(r - 2)
     pass_on(CHUNKS - 1)
-    collect(CHUNKS - 2)
-    for r in range(CHUNKS - 1):
-        finish(r)
-    collect(CHUNKS - 1)
+    for r in range(CHUNKS):
+        collect(r)
+        if 1 <= r < CHUNKS - 1:
+            finish(r - 1)
+    finish(CHUNKS - 2)
     finish(CHUNKS - 1)
 
     for way in range(2):

time: 109 us -> 106 us (0.972)
  Pallas kernels: 109 us -> 105 us
    pallas_call x1, Pallas kernels: 109 us -> 105 us  [layer(): pl.pallas_call(functools.partial(kernel, n_seq), out_shape=pltpu.VMEM((SE...]
where the time goes in v4:
time: 106 us
  Pallas kernels  105 us (99%)
    pallas_call x1, Pallas kernels, layer(): pl.pallas_call(functools.partial(kernel, n_seq), out_shape=pltpu.VMEM((SE...  105 us

profile of v4, /device:TPU:6, one launch (start us, length us, event | category | flops | bytes accessed | tf_op | source)
XLA Modules:
  0.0 105.8 jit_solution(13328971882261382581)
XLA Ops:
  0.0 105.0 %shard_map.100 = bf16[512,512]{1,0:T(8,128)(2,1)S(1)} custom-call(bf16[512,512]{1,0:T(8,128)(2,1)} %hid.1, bf16[2048,512]{1,0:T(8,128)(2,1)} %wq_in.1, bf16[2048,512]{1,0:T(8,128)(2,1)} %wk_in.1, bf16[2048,512]{1,0:T(8,128)(2,1)} %wv_in.1, bf16[2048,512]{1,0:T(8,128)(2,1)} %wp_in.1, bf16[512,2048]{1,0:T(8,128)(2,1)} %wo_in.1, f32[4,128]{1,0:T(4,128)} %bc.1, ...), custom_call_target="tpu_custom_call" | custom-call | tf_op jit(solution)/shard_map/pallas_call | solution.py:373
  105.0 0.8 copy.12

commit v5 on v4

--- a/solution.py
+++ b/solution.py
@@ -94,7 +94,7 @@
     prev_line = (lax.rem(s + n_seq - 4, n_seq), t)
 
     barrier = pltpu.get_barrier_semaphore()
-    for device in (up, down, twin, to_right, to_left, to_across, next_line, prev_line):
+    for device in (up, down, twin, next_line, prev_line):
         pl.semaphore_signal(barrier, inc=1, device_id=device, device_id_type=MESH)
 
     own_cols = pl.ds(pl.multiple_of(t * WIDTH, WIDTH), WIDTH)
@@ -195,7 +195,7 @@
     rel[3 * SEG :, :] = jnp.zeros((ROWS, WIDTH), BF16)
 
     loads[0].wait()
-    pl.semaphore_wait(barrier, 8)
+    pl.semaphore_wait(barrier, 5)
 
     projected = False
     passed, made = 0, 0
@@ -297,7 +297,7 @@
         near_l[r, HALF:, :] = (near_l[r, HALF:, :].astype(F32) + half_l[r].astype(F32)).astype(BF16)
         fin_left(r, 1).start()
 
-    others = (to_right, to_across, to_left)
+    others = (to_across, to_right, to_left)
 
     def stats_to(i, r):
         return copy_to(st_out.at[r], st_in.at[i, r], (st_s, st_r), (i, r), others[i])

time: 106 us -> 105 us (level)
  no operation moved by 1% of the time
where the time goes in v5:
time: 105 us
  Pallas kernels  105 us (100%)
    pallas_call x1, Pallas kernels, layer(): pl.pallas_call(functools.partial(kernel, n_seq), out_shape=pltpu.VMEM((SE...  105 us

profile of v5, /device:TPU:6, one launch (start us, length us, event | category | flops | bytes accessed | tf_op | source)
XLA Modules:
  0.0 105.4 jit_solution(11207764702016543376)
XLA Ops:
  0.0 104.6 %shard_map.100 = bf16[512,512]{1,0:T(8,128)(2,1)S(1)} custom-call(bf16[512,512]{1,0:T(8,128)(2,1)} %hid.1, bf16[2048,512]{1,0:T(8,128)(2,1)} %wq_in.1, bf16[2048,512]{1,0:T(8,128)(2,1)} %wk_in.1, bf16[2048,512]{1,0:T(8,128)(2,1)} %wv_in.1, bf16[2048,512]{1,0:T(8,128)(2,1)} %wp_in.1, bf16[512,2048]{1,0:T(8,128)(2,1)} %wo_in.1, f32[4,128]{1,0:T(4,128)} %bc.1, ...), custom_call_target="tpu_custom_call" | custom-call | tf_op jit(solution)/shard_map/pallas_call | solution.py:373
  104.6 0.8 copy.12
